TPU v7x, 32 devices: a whole 2x2x4 slice. The times are simulated.
32 devices in a mesh: rows: 8 (over z, y), cols: 4 (over x, core).
Axes of the slice: x: 2, y: 2, z: 4, core: 2. Of those that a mesh axis runs over, the one named last changes fastest.
Arguments:
- points: bfloat16 [4096, 256], P(('rows', 'cols')), may hold values from -6 to 6
- start_vectors: float32 [8, 4096], P(None, ('rows', 'cols')), may hold values from -6 to 6
- degree: bfloat16 [4096], P(('rows', 'cols')), may hold values from 0.19921875 to 2
Outputs:
- embedding: float32 [8, 4096], P(None, ('rows', 'cols'))
All inputs are finite; a program needn't handle non-finite values.
Results may differ from a plain program's by a relative error of at most 0.0034.
Values may be sent and summed in bfloat16 or wider, within the bound.
A program may use at most 64 MiB of HBM per device.

v0:
```python
import jax
import jax.numpy as jnp
from jax import lax
from jax.sharding import PartitionSpec as P

ITERS = 3


def body(points, start_vectors, degree):
    row_count = lax.axis_size("rows")
    col_count = lax.axis_size("cols")
    row_place = lax.axis_index("rows")
    col_place = lax.axis_index("cols")
    span_size = points.shape[0]
    sharpness = 4.0 / points.shape[1]
    row_points, row_degree = (
        lax.all_gather(points, "cols", axis=0, tiled=True),
        lax.all_gather(degree, "cols", axis=0, tiled=True),
    )
    row_total = row_points.shape[0]
    row_float = row_points.astype(jnp.float32)
    row_norms = jnp.sum(row_float * row_float, axis=1)
    row_slots = jnp.arange(row_total, dtype=jnp.int32)
    row_global = (
        row_place * col_count + row_slots // span_size
    ) * span_size + row_slots % span_size

    def kernel_block(x_block, col_norms, first_slot):
        inner = lax.dot_general(
            row_points, x_block, (((1,), (1,)), ((), ())), preferred_element_type=jnp.float32
        )
        distance = row_norms[:, None] + col_norms[None, :] - 2.0 * inner
        kernel = jnp.exp(-sharpness * distance)
        col_slots = first_slot + jnp.arange(x_block.shape[0], dtype=jnp.int32)
        col_global = (
            col_slots // span_size * col_count + col_place
        ) * span_size + col_slots % span_size
        return jnp.where(
            row_global[:, None] == col_global[None, :], jnp.float32(0.0), kernel
        ).astype(jnp.bfloat16)

    vectors = start_vectors
    for iteration in range(ITERS):
        empty = jnp.zeros((vectors.shape[0], row_total), jnp.float32)
        sending = vectors.T.astype(jnp.bfloat16)
        x_piece = lax.all_gather(points, "rows", axis=0, tiled=True)
        v_piece = lax.all_gather(sending, "rows", axis=0, tiled=True)
        piece_rows = x_piece.shape[0]
        block_size = 512
        block_count = piece_rows // block_size

        def accumulate(block_index, running):
            offset = block_index * block_size
            x_block = lax.dynamic_slice_in_dim(x_piece, offset, block_size, 0)
            v_block = lax.dynamic_slice_in_dim(v_piece, offset, block_size, 0)
            x_float = x_block.astype(jnp.float32)
            col_norms = jnp.sum(x_float * x_float, axis=1)
            kernel = kernel_block(x_block, col_norms, offset)
            return running + lax.dot_general(
                v_block, kernel, (((0,), (1,)), ((), ())), preferred_element_type=jnp.float32
            )

        partial_value = lax.fori_loop(0, block_count, accumulate, empty)
        summed = lax.psum(partial_value, "cols")
        row_state = summed / row_degree.astype(jnp.float32)[None, :]
        vectors = lax.dynamic_slice_in_dim(row_state, col_place * span_size, span_size, 1)
    magnitude = lax.psum(jnp.sum(jnp.abs(row_state), axis=1), "rows")
    mean_abs = magnitude / (span_size * row_count * col_count)
    return vectors / (mean_abs[:, None] + 1e-06)


def solution(mesh):
    return jax.shard_map(
        body,
        mesh=mesh,
        in_specs=(P(("rows", "cols"), None), P(None, ("rows", "cols")), P(("rows", "cols"))),
        out_specs=P(None, ("rows", "cols")),
        check_vma=False,
    )
```

profile of v0, /device:TPU:0, one launch (start us, length us, event | category | flops | bytes accessed | tf_op | source)
XLA Modules:
  0.0 177.6 jit_solution(2372064318550203494)
XLA Ops:
  0.0 0.0 copy-start.2
  0.0 0.7 copy-done.2
  0.7 6.0 %all-gather = bf16[4,1,128]{2,1,0:T(2,128)(2,1)S(1)} all-gather(bf16[1,1,128]{2,1,0:T(2,128)(2,1)S(1)} %bitcast.73), channel_id=1, replica_groups=mesh['rows'=8,'cols'=4] {'cols'}, dimensions={0}, use_global_device_ids=true | all-gather | bytes 1280 | tf_op jit(solution)/shard_map/all_gather | solution.py:18
  6.7 0.1 dynamic-slice
  6.7 6.5 %all_gather.21 = bf16[512,256]{1,0:T(8,128)(2,1)S(1)} all-gather(bf16[128,256]{1,0:T(8,128)(2,1)} %param.9), channel_id=1, replica_groups=mesh['rows'=8,'cols'=4] {'cols'}, dimensions={0}, use_global_device_ids=true | all-gather | bytes 327680 | tf_op jit(solution)/shard_map/all_gather | solution.py:17
  13.2 0.0 copy-start
  13.2 0.1 multiply_reduce_fusion.3
  13.4 0.7 copy-done
  14.0 0.0 copy-start.1
  14.0 32.1 %all_gather.22 = bf16[1024,256]{1,0:T(8,128)(2,1)S(1)} all-gather(bf16[128,256]{1,0:T(8,128)(2,1)S(1)} %copy-done), channel_id=1, replica_groups=mesh['rows'=8,'cols'=4] {'rows'}, dimensions={0}, use_global_device_ids=true | all-gather | bytes 589824 | tf_op jit(solution)/shard_map/all_gather | solution.py:46
  46.2 0.0 copy-done.1
  46.2 26.1 %all_gather.20 = bf16[1024,8]{0,1:T(8,128)(2,1)S(1)} all-gather(bf16[128,8]{0,1:T(8,128)(2,1)S(1)} %convert_bitcast_fusion), channel_id=1, replica_groups=mesh['rows'=8,'cols'=4] {'rows'}, dimensions={0}, use_global_device_ids=true | all-gather | bytes 18432 | tf_op jit(solution)/shard_map/all_gather | solution.py:47
  72.3 1.6 while.48
  72.3 0.1 multiply_reduce_fusion.7
  72.5 0.6 fusion.155
  73.1 0.2 multiply_reduce_fusion.7
  73.3 0.6 fusion.155
  73.9 10.1 %psum.28 = f32[8,512]{1,0:T(8,128)S(1)} all-reduce(f32[8,512]{1,0:T(8,128)S(1)} %get-tuple-element.608), channel_id=1, replica_groups=mesh['rows'=8,'cols'=4] {'cols'}, use_global_device_ids=true, to_apply=%region_4.5 | all-reduce | flops 4096 | bytes 32768 | tf_op jit(solution)/shard_map/psum | solution.py:64
  84.0 26.1 %all_gather.24 = bf16[1024,8]{0,1:T(8,128)(2,1)S(1)} all-gather(bf16[128,8]{0,1:T(8,128)(2,1)S(1)} %fusion.131), channel_id=1, replica_groups=mesh['rows'=8,'cols'=4] {'rows'}, dimensions={0}, use_global_device_ids=true | all-gather | bytes 18432 | tf_op jit(solution)/shard_map/all_gather | solution.py:47
  110.1 1.6 while.49
  110.1 0.1 multiply_reduce_fusion.8
  110.3 0.6 fusion.160
  110.9 0.2 multiply_reduce_fusion.8
  111.1 0.6 fusion.160
  111.7 10.1 %psum.29 = f32[8,512]{1,0:T(8,128)S(1)} all-reduce(f32[8,512]{1,0:T(8,128)S(1)} %get-tuple-element.609), channel_id=1, replica_groups=mesh['rows'=8,'cols'=4] {'cols'}, use_global_device_ids=true, to_apply=%region_8.9 | all-reduce | flops 4096 | bytes 32768 | tf_op jit(solution)/shard_map/psum | solution.py:64
  121.8 26.1 %all_gather.25 = bf16[1024,8]{0,1:T(8,128)(2,1)S(1)} all-gather(bf16[128,8]{0,1:T(8,128)(2,1)S(1)} %fusion.132), channel_id=1, replica_groups=mesh['rows'=8,'cols'=4] {'rows'}, dimensions={0}, use_global_device_ids=true | all-gather | bytes 18432 | tf_op jit(solution)/shard_map/all_gather | solution.py:47
  148.0 1.6 while.50
  148.0 0.1 multiply_reduce_fusion.9
  148.1 0.6 fusion.165
  148.7 0.2 multiply_reduce_fusion.9
  148.9 0.6 fusion.165
  149.5 10.1 %psum.30 = f32[8,512]{1,0:T(8,128)S(1)} all-reduce(f32[8,512]{1,0:T(8,128)S(1)} %get-tuple-element.610), channel_id=1, replica_groups=mesh['rows'=8,'cols'=4] {'cols'}, use_global_device_ids=true, to_apply=%region_12.13 | all-reduce | flops 4096 | bytes 32768 | tf_op jit(solution)/shard_map/psum | solution.py:64
  159.7 0.1 abs_reduce_fusion
  159.8 17.1 %psum.31 = f32[8]{0:T(128)S(1)} all-reduce(f32[8]{0:T(128)S(1)} %get-tuple-element.749), channel_id=1, replica_groups=mesh['rows'=8,'cols'=4] {'rows'}, use_global_device_ids=true, to_apply=%region_14.15 | all-reduce | flops 8 | bytes 64 | tf_op jit(solution)/shard_map/psum | solution.py:67
  176.9 0.7 dynamic-slice_divide_fusion.2
  (14 shorter events, 0.1 us)
Async XLA Ops:
  0.0 0.7 copy-start.2
  13.2 0.8 copy-start
  14.0 32.1 %copy-start.1 = (f32[8,128]{1,0:T(8,128)S(1)}, f32[8,128]{1,0:T(8,128)}, u32[]{:S(2)}) copy-start(f32[8,128]{1,0:T(8,128)} %param.10) | copy-start | bytes 12292
where the time goes:
time: 178 us
  blocking collectives  170 us (96%)
  matrix products  3.57 us (2%)
  other arithmetic  2.03 us (1%)
    all_gather x3, blocking collectives, body(): v_piece = lax.all_gather(sending, 'rows', axis=0, tiled=True)  78.3 us
    all_gather x1, blocking collectives, body(): x_piece = lax.all_gather(points, 'rows', axis=0, tiled=True)  32.1 us
    psum x3, blocking collectives, body(): summed = lax.psum(partial_value, 'cols')  30.4 us
    psum x1, blocking collectives, body(): magnitude = lax.psum(jnp.sum(jnp.abs(row_state), axis=1), 'rows')  17.1 us
    all_gather x1, blocking collectives, body(): lax.all_gather(points, 'cols', axis=0, tiled=True)  6.47 us
    all_gather x1, blocking collectives, body(): lax.all_gather(degree, 'cols', axis=0, tiled=True)  5.99 us
    dot_general x6, matrix products, accumulate(): lax.dot_general(v_block, kernel, (((0,), (1,)), ((), ())), preferred_elem...  3.57 us

commit v1 on v0

--- a/solution.py
+++ b/solution.py
@@ -43,7 +43,24 @@
     for iteration in range(ITERS):
         empty = jnp.zeros((vectors.shape[0], row_total), jnp.float32)
         sending = vectors.T.astype(jnp.bfloat16)
-        x_piece = lax.all_gather(points, "rows", axis=0, tiled=True)
+        length, index, rows = (lax.axis_size("rows"), lax.axis_index("rows"), points.shape[0])
+        forward = [(i, (i + 1) % length) for i in range(length)]
+        downward = [(i, (i - 1) % length) for i in range(length)]
+        out = jnp.zeros((*points.shape[:0], length * rows, *points.shape[0 + 1 :]), points.dtype)
+        out = lax.dynamic_update_slice_in_dim(out, points, index * rows, axis=0)
+        from_left = from_right = points
+        half = length // 2
+        for step in range(1, half + 1):
+            from_left = lax.ppermute(from_left, "rows", forward)
+            out = lax.dynamic_update_slice_in_dim(
+                out, from_left, (index - step) % length * rows, axis=0
+            )
+            if step < length - half:
+                from_right = lax.ppermute(from_right, "rows", downward)
+                out = lax.dynamic_update_slice_in_dim(
+                    out, from_right, (index + step) % length * rows, axis=0
+                )
+        x_piece = out
         v_piece = lax.all_gather(sending, "rows", axis=0, tiled=True)
         piece_rows = x_piece.shape[0]
         block_size = 512

time: 178 us -> 172 us (0.966)
  blocking collectives: 170 us -> 137 us
  starting transfers between devices: 0 us -> 15.5 us
  waiting for transfers between devices: 0 us -> 11.4 us
    all_gather x1 -> x0, blocking collectives: 32.1 us -> none  [body(): x_piece = lax.all_gather(points, 'rows', axis=0, tiled=True)]
    ppermute x0 -> x7, starting transfers between devices: none -> 15.5 us  [the longest x3 12.5 us: body(): from_right = lax.ppermute(from_right, 'rows', downward)]
    ppermute x0 -> x7, waiting for transfers between devices: none -> 11.4 us  [the longest x4 11.4 us: body(): from_left = lax.ppermute(from_left, 'rows', forward)]
  transfers between devices with their start and end apart: 0 -> 7, of which waited for: 0 -> 3; matrix products, arithmetic and copies ran while one was open for 0% -> 0% of each run, Pallas kernels for 0% -> 0%
where the time goes in v1:
time: 172 us
  blocking collectives  137 us (80%)
  starting transfers between devices  15.5 us (9%)
  waiting for transfers between devices  11.4 us (7%)
  matrix products  3.57 us (2%)
  local copies, waits for them, and re-layouts  2.26 us (1%)
  other arithmetic  2.04 us (1%)
    all_gather x3, blocking collectives, body(): v_piece = lax.all_gather(sending, 'rows', axis=0, tiled=True)  78.3 us
    psum x3, blocking collectives, body(): summed = lax.psum(partial_value, 'cols')  30.4 us
    psum x1, blocking collectives, body(): magnitude = lax.psum(jnp.sum(jnp.abs(row_state), axis=1), 'rows')  17.1 us
    ppermute x3, starting transfers between devices, body(): from_right = lax.ppermute(from_right, 'rows', downward)  12.5 us
    ppermute x4, waiting for transfers between devices, body(): from_left = lax.ppermute(from_left, 'rows', forward)  11.4 us
    all_gather x1, blocking collectives, body(): lax.all_gather(points, 'cols', axis=0, tiled=True)  5.89 us
    all_gather x1, blocking collectives, body(): lax.all_gather(degree, 'cols', axis=0, tiled=True)  5.05 us
    dot_general x6, matrix products, accumulate(): lax.dot_general(v_block, kernel, (((0,), (1,)), ((), ())), preferred_elem...  3.57 us
  transfers between devices with their start and end apart: 7, of which 3 were waited for; matrix products, arithmetic and copies ran while one was open for 0% of the time, Pallas kernels for 0%

profile of v1, /device:TPU:0, one launch (start us, length us, event | category | flops | bytes accessed | tf_op | source)
XLA Modules:
  0.0 171.8 jit_solution(5542084124059363002)
XLA Ops:
  0.0 3.0 %collective-permute-start = (bf16[128,256]{1,0:T(8,128)(2,1)}, bf16[128,256]{1,0:T(8,128)(2,1)S(1)}, u32[]{:S(2)}, u32[]{:S(2)}) collective-permute-start(bf16[128,256]{1,0:T(8,128)(2,1)} %param.9), channel_id=1, source_target_pairs={{0,4},{4,8},{8,12},{12,16},{16,20},{20,24},{24,28},{28,0},{1,5},{5... | collective-permute-start | bytes 196616 | tf_op jit(solution)/shard_map/ppermute | solution.py:54
  3.0 3.0 %collective-permute-start.1 = (bf16[128,256]{1,0:T(8,128)(2,1)}, bf16[128,256]{1,0:T(8,128)(2,1)S(1)}, u32[]{:S(2)}, u32[]{:S(2)}) collective-permute-start(bf16[128,256]{1,0:T(8,128)(2,1)} %param.9), channel_id=1, source_target_pairs={{0,28},{4,0},{8,4},{12,8},{16,12},{20,16},{24,20},{28,24},{1,29},{... | collective-permute-start | bytes 196616 | tf_op jit(solution)/shard_map/ppermute | solution.py:59
  6.0 0.0 copy-start
  6.0 0.9 copy-done
  6.9 5.9 %all_gather.16 = bf16[512,256]{1,0:T(8,128)(2,1)S(1)} all-gather(bf16[128,256]{1,0:T(8,128)(2,1)S(1)} %copy-done), channel_id=1, replica_groups=mesh['rows'=8,'cols'=4] {'cols'}, dimensions={0}, use_global_device_ids=true | all-gather | bytes 327680 | tf_op jit(solution)/shard_map/all_gather | solution.py:17
  12.8 0.0 copy-start.1
  12.8 0.1 multiply_reduce_fusion.3
  13.0 0.5 copy-done.1
  13.5 26.1 %all_gather.15 = bf16[1024,8]{0,1:T(8,128)(2,1)S(1)} all-gather(bf16[128,8]{0,1:T(8,128)(2,1)S(1)} %convert_bitcast_fusion), channel_id=1, replica_groups=mesh['rows'=8,'cols'=4] {'rows'}, dimensions={0}, use_global_device_ids=true | all-gather | bytes 18432 | tf_op jit(solution)/shard_map/all_gather | solution.py:64
  39.6 0.0 copy-start.2
  39.6 0.7 copy-done.2
  40.3 5.0 %all-gather = bf16[4,1,128]{2,1,0:T(2,128)(2,1)S(1)} all-gather(bf16[1,1,128]{2,1,0:T(2,128)(2,1)S(1)} %bitcast.73), channel_id=1, replica_groups=mesh['rows'=8,'cols'=4] {'cols'}, dimensions={0}, use_global_device_ids=true | all-gather | bytes 1280 | tf_op jit(solution)/shard_map/all_gather | solution.py:18
  45.3 0.1 dynamic-slice
  45.5 0.0 collective-permute-done
  45.5 0.1 collective-permute-start.2
  45.5 0.0 collective-permute-done.1
  45.5 4.7 %collective-permute-start.3 = (bf16[128,256]{1,0:T(8,128)(2,1)S(1)}, bf16[128,256]{1,0:T(8,128)(2,1)S(1)}, u32[]{:S(2)}, u32[]{:S(2)}) collective-permute-start(bf16[128,256]{1,0:T(8,128)(2,1)S(1)} %collective-permute-done.1), channel_id=1, source_target_pairs={{0,28},{4,0},{8,4},{12,8},{16,12},{20,16},{24,20},{28,24},{1,29},{... | collective-permute-start | bytes 196616 | tf_op jit(solution)/shard_map/ppermute | solution.py:59
  50.3 2.3 %collective-permute-done.2 = bf16[128,256]{1,0:T(8,128)(2,1)S(1)} collective-permute-done((bf16[128,256]{1,0:T(8,128)(2,1)S(1)}, bf16[128,256]{1,0:T(8,128)(2,1)S(1)}, u32[]{:S(2)}, u32[]{:S(2)}) %collective-permute-start.2) | collective-permute-done | bytes 65568 | tf_op jit(solution)/shard_map/ppermute | solution.py:54
  52.6 0.0 collective-permute-start.4
  52.6 0.0 collective-permute-done.3
  52.6 4.7 %collective-permute-start.5 = (bf16[128,256]{1,0:T(8,128)(2,1)S(1)}, bf16[128,256]{1,0:T(8,128)(2,1)S(1)}, u32[]{:S(2)}, u32[]{:S(2)}) collective-permute-start(bf16[128,256]{1,0:T(8,128)(2,1)S(1)} %collective-permute-done.3), channel_id=1, source_target_pairs={{0,28},{4,0},{8,4},{12,8},{16,12},{20,16},{24,20},{28,24},{1,29},{... | collective-permute-start | bytes 196616 | tf_op jit(solution)/shard_map/ppermute | solution.py:59
  57.3 2.2 %collective-permute-done.4 = bf16[128,256]{1,0:T(8,128)(2,1)S(1)} collective-permute-done((bf16[128,256]{1,0:T(8,128)(2,1)S(1)}, bf16[128,256]{1,0:T(8,128)(2,1)S(1)}, u32[]{:S(2)}, u32[]{:S(2)}) %collective-permute-start.4) | collective-permute-done | bytes 65568 | tf_op jit(solution)/shard_map/ppermute | solution.py:54
  59.5 0.0 collective-permute-start.6
  59.5 0.0 collective-permute-done.5
  59.6 6.9 %collective-permute-done.6 = bf16[128,256]{1,0:T(8,128)(2,1)S(1)} collective-permute-done((bf16[128,256]{1,0:T(8,128)(2,1)S(1)}, bf16[128,256]{1,0:T(8,128)(2,1)S(1)}, u32[]{:S(2)}, u32[]{:S(2)}) %collective-permute-start.6) | collective-permute-done | bytes 65568 | tf_op jit(solution)/shard_map/ppermute | solution.py:54
  66.5 1.6 while.48
  66.5 0.2 multiply_reduce_fusion.7
  66.7 0.6 fusion.155
  67.3 0.2 multiply_reduce_fusion.7
  67.5 0.6 fusion.155
  68.1 10.1 %psum.28 = f32[8,512]{1,0:T(8,128)S(1)} all-reduce(f32[8,512]{1,0:T(8,128)S(1)} %get-tuple-element.608), channel_id=1, replica_groups=mesh['rows'=8,'cols'=4] {'cols'}, use_global_device_ids=true, to_apply=%region_4.5 | all-reduce | flops 4096 | bytes 32768 | tf_op jit(solution)/shard_map/psum | solution.py:81
  78.2 26.1 %all_gather.18 = bf16[1024,8]{0,1:T(8,128)(2,1)S(1)} all-gather(bf16[128,8]{0,1:T(8,128)(2,1)S(1)} %fusion.131), channel_id=1, replica_groups=mesh['rows'=8,'cols'=4] {'rows'}, dimensions={0}, use_global_device_ids=true | all-gather | bytes 18432 | tf_op jit(solution)/shard_map/all_gather | solution.py:64
  104.3 1.6 while.49
  104.3 0.1 multiply_reduce_fusion.8
  104.5 0.6 fusion.160
  105.1 0.2 multiply_reduce_fusion.8
  105.3 0.6 fusion.160
  105.9 10.1 %psum.29 = f32[8,512]{1,0:T(8,128)S(1)} all-reduce(f32[8,512]{1,0:T(8,128)S(1)} %get-tuple-element.609), channel_id=1, replica_groups=mesh['rows'=8,'cols'=4] {'cols'}, use_global_device_ids=true, to_apply=%region_8.9 | all-reduce | flops 4096 | bytes 32768 | tf_op jit(solution)/shard_map/psum | solution.py:81
  116.0 26.1 %all_gather.19 = bf16[1024,8]{0,1:T(8,128)(2,1)S(1)} all-gather(bf16[128,8]{0,1:T(8,128)(2,1)S(1)} %fusion.132), channel_id=1, replica_groups=mesh['rows'=8,'cols'=4] {'rows'}, dimensions={0}, use_global_device_ids=true | all-gather | bytes 18432 | tf_op jit(solution)/shard_map/all_gather | solution.py:64
  142.2 1.6 while.50
  142.2 0.1 multiply_reduce_fusion.9
  142.3 0.6 fusion.165
  142.9 0.2 multiply_reduce_fusion.9
  143.1 0.6 fusion.165
  143.7 10.1 %psum.30 = f32[8,512]{1,0:T(8,128)S(1)} all-reduce(f32[8,512]{1,0:T(8,128)S(1)} %get-tuple-element.610), channel_id=1, replica_groups=mesh['rows'=8,'cols'=4] {'cols'}, use_global_device_ids=true, to_apply=%region_12.13 | all-reduce | flops 4096 | bytes 32768 | tf_op jit(solution)/shard_map/psum | solution.py:81
  153.9 0.1 abs_reduce_fusion
  154.0 17.1 %psum.31 = f32[8]{0:T(128)S(1)} all-reduce(f32[8]{0:T(128)S(1)} %get-tuple-element.749), channel_id=1, replica_groups=mesh['rows'=8,'cols'=4] {'rows'}, use_global_device_ids=true, to_apply=%region_14.15 | all-reduce | flops 8 | bytes 64 | tf_op jit(solution)/shard_map/psum | solution.py:84
  171.1 0.7 dynamic-slice_divide_fusion.2
  (23 shorter events, 0.2 us)
Async XLA Ops:
  0.0 45.5 %collective-permute-start = (bf16[128,256]{1,0:T(8,128)(2,1)}, bf16[128,256]{1,0:T(8,128)(2,1)S(1)}, u32[]{:S(2)}, u32[]{:S(2)}) collective-permute-start(bf16[128,256]{1,0:T(8,128)(2,1)} %param.9), channel_id=1, source_target_pairs={{0,4},{4,8},{8,12},{12,16},{16,20},{20,24},{24,28},{28,0},{1,5},{5... | collective-permute-start | bytes 196616 | tf_op jit(solution)/shard_map/ppermute | solution.py:54
  3.0 42.5 %collective-permute-start.1 = (bf16[128,256]{1,0:T(8,128)(2,1)}, bf16[128,256]{1,0:T(8,128)(2,1)S(1)}, u32[]{:S(2)}, u32[]{:S(2)}) collective-permute-start(bf16[128,256]{1,0:T(8,128)(2,1)} %param.9), channel_id=1, source_target_pairs={{0,28},{4,0},{8,4},{12,8},{16,12},{20,16},{24,20},{28,24},{1,29},{... | collective-permute-start | bytes 196616 | tf_op jit(solution)/shard_map/ppermute | solution.py:59
  6.0 0.9 copy-start
  12.8 0.7 copy-start.1
  39.6 0.7 copy-start.2
  45.5 7.1 %collective-permute-start.2 = (bf16[128,256]{1,0:T(8,128)(2,1)S(1)}, bf16[128,256]{1,0:T(8,128)(2,1)S(1)}, u32[]{:S(2)}, u32[]{:S(2)}) collective-permute-start(bf16[128,256]{1,0:T(8,128)(2,1)S(1)} %collective-permute-done), channel_id=1, source_target_pairs={{0,4},{4,8},{8,12},{12,16},{16,20},{20,24},{24,28},{28,0},{1,5},{5... | collective-permute-start | bytes 196616 | tf_op jit(solution)/shard_map/ppermute | solution.py:54
  45.5 7.0 %collective-permute-start.3 = (bf16[128,256]{1,0:T(8,128)(2,1)S(1)}, bf16[128,256]{1,0:T(8,128)(2,1)S(1)}, u32[]{:S(2)}, u32[]{:S(2)}) collective-permute-start(bf16[128,256]{1,0:T(8,128)(2,1)S(1)} %collective-permute-done.1), channel_id=1, source_target_pairs={{0,28},{4,0},{8,4},{12,8},{16,12},{20,16},{24,20},{28,24},{1,29},{... | collective-permute-start | bytes 196616 | tf_op jit(solution)/shard_map/ppermute | solution.py:59
  52.6 7.0 %collective-permute-start.4 = (bf16[128,256]{1,0:T(8,128)(2,1)S(1)}, bf16[128,256]{1,0:T(8,128)(2,1)S(1)}, u32[]{:S(2)}, u32[]{:S(2)}) collective-permute-start(bf16[128,256]{1,0:T(8,128)(2,1)S(1)} %collective-permute-done.2), channel_id=1, source_target_pairs={{0,4},{4,8},{8,12},{12,16},{16,20},{20,24},{24,28},{28,0},{1,5},{5... | collective-permute-start | bytes 196616 | tf_op jit(solution)/shard_map/ppermute | solution.py:54
  52.6 7.0 %collective-permute-start.5 = (bf16[128,256]{1,0:T(8,128)(2,1)S(1)}, bf16[128,256]{1,0:T(8,128)(2,1)S(1)}, u32[]{:S(2)}, u32[]{:S(2)}) collective-permute-start(bf16[128,256]{1,0:T(8,128)(2,1)S(1)} %collective-permute-done.3), channel_id=1, source_target_pairs={{0,28},{4,0},{8,4},{12,8},{16,12},{20,16},{24,20},{28,24},{1,29},{... | collective-permute-start | bytes 196616 | tf_op jit(solution)/shard_map/ppermute | solution.py:59
  59.5 7.0 %collective-permute-start.6 = (bf16[128,256]{1,0:T(8,128)(2,1)S(1)}, bf16[128,256]{1,0:T(8,128)(2,1)S(1)}, u32[]{:S(2)}, u32[]{:S(2)}) collective-permute-start(bf16[128,256]{1,0:T(8,128)(2,1)S(1)} %collective-permute-done.4), channel_id=1, source_target_pairs={{0,4},{4,8},{8,12},{12,16},{16,20},{20,24},{24,28},{28,0},{1,5},{5... | collective-permute-start | bytes 196616 | tf_op jit(solution)/shard_map/ppermute | solution.py:54
